TPU v7x, 32 devices: a whole 2x2x4 slice. The times are simulated.
32 devices in a mesh: pp: 2 (over core), ep: 16 (over z, y, x), tp: 1.
Axes of the slice: x: 2, y: 2, z: 4, core: 2. Of those that a mesh axis runs over, the one named last changes fastest.
Arguments:
- acts: bfloat16 [2, 96, 3072], P(None, 'ep'), may hold values from -6 to 6
- route_ids: int32 [2, 2, 96, 8], P('pp', None, 'ep'), may hold values from 0 to 23, all different within a row; in each aligned block of 6 rows (0 to 5, 6 to 11, ..., all dimensions but the last counted through in order) at most 2 rows name the same one
- norm_gain: bfloat16 [2, 3072], P('pp'), may hold values from 0.5 to 1.5
- router: bfloat16 [2, 3072, 24], P('pp'), may hold values from -0.109375 to 0.109375
- dense_gate: bfloat16 [2, 3072, 6144], P('pp', None, ('ep', 'tp')), may hold values from -0.109375 to 0.109375
- dense_up: bfloat16 [2, 3072, 6144], P('pp', None, ('ep', 'tp')), may hold values from -0.109375 to 0.109375
- dense_down: bfloat16 [2, 6144, 3072], P('pp', ('ep', 'tp')), may hold values from -0.078125 to 0.078125
- expert_gate: bfloat16 [2, 16, 3072, 1024], P('pp', 'ep', None, 'tp'), may hold values from -0.109375 to 0.109375
- expert_up: bfloat16 [2, 16, 3072, 1024], P('pp', 'ep', None, 'tp'), may hold values from -0.109375 to 0.109375
- expert_down: bfloat16 [2, 16, 1024, 3072], P('pp', 'ep', 'tp'), may hold values from -0.1875 to 0.1875
Outputs:
- layer_out: bfloat16 [2, 2, 96, 3072], P('pp', None, 'ep')
Inputs may be any that keep to these rules, and one draw needn't show every extreme that they name: `route_ids`: the 8 ids of a token differ. In each layer and microbatch, among the 6 tokens of one ep index no id is named by more than 2 tokens, a bound that some block reaches.
All inputs are finite; a program needn't handle non-finite values.
Results may differ from a plain program's by a relative error of at most 0.008.
Values may be sent and summed in bfloat16 or wider, within the bound.
No kernel may reach another device: no remote copies, remote signals or barrier semaphores. Data moves between devices by JAX's collectives and lax.ppermute only.
A program may use at most 128 MiB of HBM per device.

v0:
```python
import jax
import jax.numpy as jnp
from jax import lax
from jax.sharding import PartitionSpec as P


def from_behind(block, axis, distance):
    devices = range(lax.axis_size(axis))
    route = [(i - distance, i) for i in devices if i - distance in devices]
    return lax.ppermute(block, axis, route)


def normalize(inputs, gain):
    widened = inputs.astype(jnp.float32)
    spread = jnp.mean(widened * widened, axis=-1, keepdims=True)
    normed = (widened * lax.rsqrt(spread + 1e-06) * gain.astype(jnp.float32)).astype(jnp.bfloat16)
    return (widened, normed)


def gated_block(inputs, w_gate, w_up, w_down):
    gate_part = jnp.dot(inputs, w_gate, preferred_element_type=jnp.float32)
    up_part = jnp.dot(inputs, w_up, preferred_element_type=jnp.float32)
    hidden = (jax.nn.silu(gate_part) * up_part).astype(jnp.bfloat16)
    return jnp.dot(hidden, w_down, preferred_element_type=jnp.float32)


def choice_weights(normed, route_rows, router_w, n_real):
    n_total = router_w.shape[1]
    gates = jax.nn.sigmoid(jnp.dot(normed, router_w, preferred_element_type=jnp.float32))
    picked = (route_rows[:, :, None] == jnp.arange(n_total, dtype=jnp.int32)[None, None, :]).astype(
        jnp.float32
    )
    weights = jnp.sum(picked * gates[:, None, :], axis=-1)
    zero_share = jnp.sum(jnp.where(route_rows >= n_real, weights, jnp.float32(0.0)), axis=-1)
    return (weights, picked, zero_share)


def on_device(
    acts,
    route_ids,
    norm_gain,
    router,
    dense_gate,
    dense_up,
    dense_down,
    expert_gate,
    expert_up,
    expert_down,
):
    n_micro, per_group, width = acts.shape
    top_count = route_ids.shape[-1]
    n_groups = lax.axis_size("ep")
    n_pairs = lax.axis_size("tp")
    section = lax.axis_index("pp")
    group_pos = lax.axis_index("ep")
    pair_pos = lax.axis_index("tp")
    micro_rows = per_group * n_groups
    share = per_group // n_pairs
    gain = norm_gain[0]
    router_w = router[0]
    total_ids = router_w.shape[1]
    slot_count = max(2, (per_group * top_count + total_ids - 1) // total_ids)
    d_gate = dense_gate[0]
    d_up = dense_up[0]
    d_down = dense_down[0]
    e_gate = expert_gate[0, 0]
    e_up = expert_up[0, 0]
    e_down = expert_down[0, 0]
    slot_range = jnp.arange(slot_count, dtype=jnp.float32)
    incoming = jnp.zeros((per_group, width), jnp.bfloat16)
    outputs = jnp.zeros((n_micro, per_group, width), jnp.bfloat16)
    for tick_index in range(n_micro + 1):
        local_micro = tick_index - section
        micro_index = jnp.clip(local_micro, 0, n_micro - 1)
        valid = jnp.logical_and(local_micro >= 0, local_micro < n_micro)
        first_input = acts[min(tick_index, n_micro - 1)]
        current = jnp.where(section == 0, first_input, incoming)
        route_rows = lax.dynamic_index_in_dim(route_ids[0], micro_index, 0, keepdims=False)
        widened, normed = normalize(current, gain)
        weights, picked, zero_share = choice_weights(normed, route_rows, router_w, n_groups)
        all_normed = lax.all_gather(normed, "ep", axis=0, tiled=True)
        real_pick = picked[:, :, :n_groups]
        hot = jnp.sum(real_pick, axis=1)
        coef = jnp.einsum("tk,tke->te", weights, real_pick, precision=lax.Precision.HIGHEST)
        position = jnp.cumsum(hot, axis=0) - hot
        select = hot.T[:, None, :] * (position.T[:, None, :] == slot_range[None, :, None]).astype(
            jnp.float32
        )
        outgoing = jnp.einsum(
            "esi,id->esd", select.astype(jnp.bfloat16), normed, preferred_element_type=jnp.float32
        ).astype(jnp.bfloat16)
        received = lax.all_to_all(outgoing, "ep", split_axis=0, concat_axis=0, tiled=True)
        flat = received.reshape(-1, width)
        produced = gated_block(flat, e_gate, e_up, e_down).reshape(received.shape[:-1] + (width,))
        returned = lax.all_to_all(produced, "ep", split_axis=0, concat_axis=0, tiled=True)
        own_rows = jnp.einsum(
            "esi,esd->id", select * coef.T[:, None, :], returned, precision=lax.Precision.HIGHEST
        )
        extra = lax.dynamic_update_slice_in_dim(
            jnp.zeros((micro_rows, width), jnp.float32), own_rows, group_pos * per_group, 0
        )
        summed = lax.psum_scatter(
            gated_block(all_normed, d_gate, d_up, d_down) + extra,
            ("ep", "tp"),
            scatter_dimension=0,
            tiled=True,
        )
        offset = pair_pos * share
        own_inputs = lax.dynamic_slice_in_dim(widened, offset, share, 0)
        own_normed = lax.dynamic_slice_in_dim(normed, offset, share, 0).astype(jnp.float32)
        own_zero = lax.dynamic_slice_in_dim(zero_share, offset, share, 0)
        result_part = (own_inputs + summed + own_zero[:, None] * own_normed).astype(jnp.bfloat16)
        finished = lax.all_gather(result_part, "tp", axis=0, tiled=True)
        updated = lax.dynamic_update_index_in_dim(outputs, finished, micro_index, 0)
        outputs = jnp.where(valid, updated, outputs)
        if tick_index < n_micro:
            incoming = from_behind(finished, "pp", 1)
    return outputs[None]


def solution(mesh):
    return jax.shard_map(
        on_device,
        mesh=mesh,
        in_specs=(
            P(None, "ep", None),
            P("pp", None, "ep", None),
            P("pp", None),
            P("pp", None, None),
            P("pp", None, ("ep", "tp")),
            P("pp", None, ("ep", "tp")),
            P("pp", ("ep", "tp"), None),
            P("pp", "ep", None, "tp"),
            P("pp", "ep", None, "tp"),
            P("pp", "ep", "tp", None),
        ),
        out_specs=P("pp", None, "ep", None),
        check_vma=False,
    )
```

profile of v0, /device:TPU:0, one launch (start us, length us, event | category | flops | bytes accessed | tf_op | source)
XLA Modules:
  0.0 461.7 jit_solution(911177788010176452)
XLA Ops:
  1.0 1.7 fusion.201
  4.8 8.3 %all-to-all-start = ((bf16[16,2,3072]{2,1,0:T(2,128)(2,1)}), bf16[16,2,3072]{2,1,0:T(2,128)(2,1)S(1)}, u32[]{:S(2)}, u32[]{:S(2)}) async-start(bf16[16,2,3072]{2,1,0:T(2,128)(2,1)} %copy.46), calls=%async_computation | async-start | bytes 393216 | tf_op jit(solution)/shard_map/all_to_all | solution.py:92
  13.2 1.1 fusion.92
  15.1 48.1 %all-gather = bf16[16,6,3072]{2,1,0:T(8,128)(2,1)} all-gather(bf16[1,6,3072]{2,1,0:T(8,128)(2,1)S(1)} %fusion.192), channel_id=1, replica_groups=mesh['pp'=2,'ep'=16,'tp'=1] {'ep'}, dimensions={0}, use_global_device_ids=true | all-gather | bytes 626688 | tf_op jit(solution)/shard_map/all_gather | solution.py:81
  63.3 4.1 fusion.19
  67.9 1.2 fusion.75
  69.2 4.0 fusion.7
  73.1 1.1 copy.48
  74.2 3.6 all-to-all-start.1
  78.4 1.3 reshape.94
  81.0 2.9 fusion.40
  83.9 3.8 fusion.28
  87.7 1.4 fusion.23
  89.1 1.6 add.116
  90.7 50.0 %fusion = f32[8,3072]{1,0:T(8,128)S(1)} fusion(f32[96,3072]{1,0:T(8,128)} %add.116), kind=kCustom, calls=%all-reduce-scatter | all-reduce-scatter fusion | flops 393217 | bytes 1278464
  140.7 1.8 collective-permute-start.2
  142.5 1.3 collective-permute-start.3
  143.8 5.1 %collective-permute-start.4 = (f32[8,3072]{1,0:T(8,128)S(1)}, f32[8,3072]{1,0:T(8,128)S(1)}, u32[]{:S(2)}, u32[]{:S(2)}) collective-permute-start(f32[8,3072]{1,0:T(8,128)S(1)} %fusion), channel_id=1, source_target_pairs={{0,3},{1,4},{2,5},{3,6},{4,7},{5,8},{6,9},{7,10},{8,11},{9,12},{10... | collective-permute-start | bytes 294920
  148.9 3.3 collective-permute-start.5
  152.9 1.4 collective-permute-done.5
  155.7 1.3 collective-permute-start
  159.0 1.1 fusion.89
  161.3 4.7 %all-to-all-start.2 = ((bf16[16,2,3072]{2,1,0:T(2,128)(2,1)}), bf16[16,2,3072]{2,1,0:T(2,128)(2,1)S(1)}, u32[]{:S(2)}, u32[]{:S(2)}) async-start(bf16[16,2,3072]{2,1,0:T(2,128)(2,1)} %copy.52), calls=%async_computation.2 | async-start | bytes 393216 | tf_op jit(solution)/shard_map/all_to_all | solution.py:92
  166.1 48.3 %all-gather.1 = bf16[16,6,3072]{2,1,0:T(8,128)(2,1)} all-gather(bf16[1,6,3072]{2,1,0:T(8,128)(2,1)S(1)} %fusion.198), channel_id=1, replica_groups=mesh['pp'=2,'ep'=16,'tp'=1] {'ep'}, dimensions={0}, use_global_device_ids=true | all-gather | bytes 626688 | tf_op jit(solution)/shard_map/all_gather | solution.py:81
  214.5 4.0 fusion.17
  218.5 4.0 fusion.72
  222.5 4.0 fusion.5
  226.4 1.1 copy.54
  227.5 3.7 all-to-all-start.3
  231.4 1.3 reshape.96
  232.8 2.8 fusion.38
  235.6 3.8 fusion.26
  239.5 1.4 all-to-all-done.3
  240.9 1.3 fusion.22
  242.2 1.6 add.123
  243.9 49.4 %fusion.1 = f32[8,3072]{1,0:T(8,128)S(1)} fusion(f32[96,3072]{1,0:T(8,128)} %add.123), kind=kCustom, calls=%all-reduce-scatter.1 | all-reduce-scatter fusion | flops 393217 | bytes 1278464
  293.3 1.3 collective-permute-start.6
  294.6 1.3 collective-permute-start.7
  295.9 4.6 collective-permute-start.8
  300.5 2.8 collective-permute-start.9
  303.4 2.1 collective-permute-done.9
  306.1 2.4 concatenate.1
  308.6 1.3 collective-permute-start.1
  310.9 1.1 fusion.86
  313.3 5.3 %all-to-all-start.4 = ((bf16[16,2,3072]{2,1,0:T(2,128)(2,1)}), bf16[16,2,3072]{2,1,0:T(2,128)(2,1)S(1)}, u32[]{:S(2)}, u32[]{:S(2)}) async-start(bf16[16,2,3072]{2,1,0:T(2,128)(2,1)} %copy.57), calls=%async_computation.4 | async-start | bytes 393216 | tf_op jit(solution)/shard_map/all_to_all | solution.py:92
  318.8 48.3 %all-gather.2 = bf16[16,6,3072]{2,1,0:T(8,128)(2,1)} all-gather(bf16[1,6,3072]{2,1,0:T(8,128)(2,1)S(1)} %fusion.195), channel_id=1, replica_groups=mesh['pp'=2,'ep'=16,'tp'=1] {'ep'}, dimensions={0}, use_global_device_ids=true | all-gather | bytes 626688 | tf_op jit(solution)/shard_map/all_gather | solution.py:81
  367.1 4.0 fusion.15
  371.1 4.0 fusion.69
  375.1 4.0 fusion.3
  379.1 1.1 copy.59
  380.2 3.6 all-to-all-start.5
  383.9 1.3 reshape.98
  385.2 2.9 fusion.36
  388.1 3.8 fusion.24
  391.9 1.4 all-to-all-done.5
  393.3 1.3 fusion.21
  394.7 1.6 add.130
  396.3 49.4 %fusion.2 = f32[8,3072]{1,0:T(8,128)S(1)} fusion(f32[96,3072]{1,0:T(8,128)} %add.130), kind=kCustom, calls=%all-reduce-scatter.2 | all-reduce-scatter fusion | flops 393217 | bytes 1278464
  445.7 1.3 collective-permute-start.10
  447.0 1.3 collective-permute-start.11
  448.3 4.6 collective-permute-start.12
  452.9 2.7 collective-permute-start.13
  455.8 2.1 collective-permute-done.13
  458.5 2.4 concatenate.2
  (101 shorter events, 16.5 us)
Async XLA Ops:
  0.0 83.9 %copy-start = (bf16[1,384,3072]{2,1,0:T(8,128)(2,1)S(1)}, bf16[1,384,3072]{2,1,0:T(8,128)(2,1)}, u32[]{:S(2)}) copy-start(bf16[1,384,3072]{2,1,0:T(8,128)(2,1)} %param.16) | copy-start | bytes 7077892
  2.9 10.3 %copy-start.9 = (f32[6]{0:T(128)}, f32[6]{0:T(128)S(1)}, u32[]{:S(2)}) copy-start(f32[6]{0:T(128)S(1)} %add_rsqrt_fusion.2) | copy-start | bytes 76
  4.8 58.4 %all-to-all-start = ((bf16[16,2,3072]{2,1,0:T(2,128)(2,1)}), bf16[16,2,3072]{2,1,0:T(2,128)(2,1)S(1)}, u32[]{:S(2)}, u32[]{:S(2)}) async-start(bf16[16,2,3072]{2,1,0:T(2,128)(2,1)} %copy.46), calls=%async_computation | async-start | bytes 393216 | tf_op jit(solution)/shard_map/all_to_all | solution.py:92
  14.5 0.6 copy-start.6
  63.3 4.6 copy-start.1
  73.1 6.7 %copy-start.12 = (u32[32]{0:T(128)S(1)}, u32[32]{0:T(128)}, u32[]{:S(2)}) copy-start(u32[32]{0:T(128)} %constant.91) | copy-start | bytes 388
  74.2 13.5 %all-to-all-start.1 = ((f32[16,2,3072]{2,1,0:T(2,128)}), f32[16,2,3072]{2,1,0:T(2,128)S(1)}, u32[]{:S(2)}, u32[]{:S(2)}) async-start(f32[16,2,3072]{2,1,0:T(2,128)} %copy.48), calls=%async_computation.1 | async-start | bytes 786432 | tf_op jit(solution)/shard_map/all_to_all | solution.py:95
  140.7 13.7 %collective-permute-start.2 = (f32[8,3072]{1,0:T(8,128)S(1)}, f32[8,3072]{1,0:T(8,128)S(1)}, u32[]{:S(2)}, u32[]{:S(2)}) collective-permute-start(f32[8,3072]{1,0:T(8,128)S(1)} %fusion), channel_id=1, source_target_pairs={{0,1},{1,2},{2,3},{3,4},{4,5},{5,6},{6,7},{7,8},{8,9},{9,10},{10,1... | collective-permute-start | bytes 294920
  142.5 11.9 %collective-permute-start.3 = (f32[8,3072]{1,0:T(8,128)S(1)}, f32[8,3072]{1,0:T(8,128)S(1)}, u32[]{:S(2)}, u32[]{:S(2)}) collective-permute-start(f32[8,3072]{1,0:T(8,128)S(1)} %fusion), channel_id=1, source_target_pairs={{0,2},{1,3},{2,4},{3,5},{4,6},{5,7},{6,8},{7,9},{8,10},{9,11},{10,... | collective-permute-start | bytes 294920
  143.8 10.6 %collective-permute-start.4 = (f32[8,3072]{1,0:T(8,128)S(1)}, f32[8,3072]{1,0:T(8,128)S(1)}, u32[]{:S(2)}, u32[]{:S(2)}) collective-permute-start(f32[8,3072]{1,0:T(8,128)S(1)} %fusion), channel_id=1, source_target_pairs={{0,3},{1,4},{2,5},{3,6},{4,7},{5,8},{6,9},{7,10},{8,11},{9,12},{10... | collective-permute-start | bytes 294920
  148.9 5.5 %collective-permute-start.5 = (f32[6,3072]{1,0:T(8,128)S(1)}, f32[6,3072]{1,0:T(8,128)S(1)}, u32[]{:S(2)}, u32[]{:S(2)}) collective-permute-start(f32[6,3072]{1,0:T(8,128)S(1)} %slice.36), channel_id=1, source_target_pairs={{0,4},{1,5},{2,6},{3,7},{4,8},{5,9},{6,10},{7,11},{8,12},{9,13},{1... | collective-permute-start | bytes 221192
  155.7 2.2 collective-permute-start
  158.9 2.4 copy-start.10
  161.3 53.1 %all-to-all-start.2 = ((bf16[16,2,3072]{2,1,0:T(2,128)(2,1)}), bf16[16,2,3072]{2,1,0:T(2,128)(2,1)S(1)}, u32[]{:S(2)}, u32[]{:S(2)}) async-start(bf16[16,2,3072]{2,1,0:T(2,128)(2,1)} %copy.52), calls=%async_computation.2 | async-start | bytes 393216 | tf_op jit(solution)/shard_map/all_to_all | solution.py:92
  166.1 65.1 %copy-start.7 = (f32[6,8]{1,0:T(8,128)}, f32[6,8]{1,0:T(8,128)S(1)}, u32[]{:S(2)}) copy-start(f32[6,8]{1,0:T(8,128)S(1)} %select_reduce_fusion.1) | copy-start | bytes 580
  227.5 13.3 %all-to-all-start.3 = ((f32[16,2,3072]{2,1,0:T(2,128)}), f32[16,2,3072]{2,1,0:T(2,128)S(1)}, u32[]{:S(2)}, u32[]{:S(2)}) async-start(f32[16,2,3072]{2,1,0:T(2,128)} %copy.54), calls=%async_computation.3 | async-start | bytes 786432 | tf_op jit(solution)/shard_map/all_to_all | solution.py:95
  235.6 67.6 %copy-start.8 = (f32[6,8]{1,0:T(8,128)S(1)}, f32[6,8]{1,0:T(8,128)}, u32[]{:S(2)}) copy-start(f32[6,8]{1,0:T(8,128)} %copy-done.7) | copy-start | bytes 580
  239.5 69.0 %copy-start.11 = (f32[6]{0:T(128)S(1)}, f32[6]{0:T(128)}, u32[]{:S(2)}) copy-start(f32[6]{0:T(128)} %copy-done.10) | copy-start | bytes 76
  242.2 68.5 %copy-start.2 = (bf16[1,6,3072]{2,0,1:T(2,128)(2,1)S(1)}, bf16[1,6,3072]{2,0,1:T(2,128)(2,1)}, u32[]{:S(2)}) copy-start(bf16[1,6,3072]{2,0,1:T(2,128)(2,1)} %get-tuple-element.15) | copy-start | bytes 110596
  293.3 12.2 %collective-permute-start.6 = (f32[8,3072]{1,0:T(8,128)S(1)}, f32[8,3072]{1,0:T(8,128)S(1)}, u32[]{:S(2)}, u32[]{:S(2)}) collective-permute-start(f32[8,3072]{1,0:T(8,128)S(1)} %fusion.1), channel_id=1, source_target_pairs={{0,1},{1,2},{2,3},{3,4},{4,5},{5,6},{6,7},{7,8},{8,9},{9,10},{10,1... | collective-permute-start | bytes 294920
  294.6 10.9 %collective-permute-start.7 = (f32[8,3072]{1,0:T(8,128)S(1)}, f32[8,3072]{1,0:T(8,128)S(1)}, u32[]{:S(2)}, u32[]{:S(2)}) collective-permute-start(f32[8,3072]{1,0:T(8,128)S(1)} %fusion.1), channel_id=1, source_target_pairs={{0,2},{1,3},{2,4},{3,5},{4,6},{5,7},{6,8},{7,9},{8,10},{9,11},{10,... | collective-permute-start | bytes 294920
  295.9 10.2 %collective-permute-start.8 = (f32[8,3072]{1,0:T(8,128)S(1)}, f32[8,3072]{1,0:T(8,128)}, u32[]{:S(2)}, u32[]{:S(2)}) collective-permute-start(f32[8,3072]{1,0:T(8,128)S(1)} %fusion.1), channel_id=1, source_target_pairs={{0,3},{1,4},{2,5},{3,6},{4,7},{5,8},{6,9},{7,10},{8,11},{9,12},{10... | collective-permute-start | bytes 294920
  300.5 5.0 %collective-permute-start.9 = (f32[6,3072]{1,0:T(8,128)S(1)}, f32[6,3072]{1,0:T(8,128)S(1)}, u32[]{:S(2)}, u32[]{:S(2)}) collective-permute-start(f32[6,3072]{1,0:T(8,128)S(1)} %slice.37), channel_id=1, source_target_pairs={{0,4},{1,5},{2,6},{3,7},{4,8},{5,9},{6,10},{7,11},{8,12},{9,13},{1... | collective-permute-start | bytes 221192
  305.4 0.6 copy-start.4
  308.6 2.2 collective-permute-start.1
  313.3 53.8 %all-to-all-start.4 = ((bf16[16,2,3072]{2,1,0:T(2,128)(2,1)}), bf16[16,2,3072]{2,1,0:T(2,128)(2,1)S(1)}, u32[]{:S(2)}, u32[]{:S(2)}) async-start(bf16[16,2,3072]{2,1,0:T(2,128)(2,1)} %copy.57), calls=%async_computation.4 | async-start | bytes 393216 | tf_op jit(solution)/shard_map/all_to_all | solution.py:92
  380.2 13.2 %all-to-all-start.5 = ((f32[16,2,3072]{2,1,0:T(2,128)}), f32[16,2,3072]{2,1,0:T(2,128)S(1)}, u32[]{:S(2)}, u32[]{:S(2)}) async-start(f32[16,2,3072]{2,1,0:T(2,128)} %copy.59), calls=%async_computation.5 | async-start | bytes 786432 | tf_op jit(solution)/shard_map/all_to_all | solution.py:95
  394.7 66.2 %copy-start.3 = (bf16[1,2,6,3072]{3,2,1,0:T(8,128)(2,1)S(1)}, bf16[1,2,6,3072]{3,2,1,0:T(8,128)(2,1)}, u32[]{:S(2)}) copy-start(bf16[1,2,6,3072]{3,2,1,0:T(8,128)(2,1)} %copy.121) | copy-start | bytes 221188
  445.7 12.1 %collective-permute-start.10 = (f32[8,3072]{1,0:T(8,128)S(1)}, f32[8,3072]{1,0:T(8,128)S(1)}, u32[]{:S(2)}, u32[]{:S(2)}) collective-permute-start(f32[8,3072]{1,0:T(8,128)S(1)} %fusion.2), channel_id=1, source_target_pairs={{0,1},{1,2},{2,3},{3,4},{4,5},{5,6},{6,7},{7,8},{8,9},{9,10},{10,1... | collective-permute-start | bytes 294920
  447.0 10.8 %collective-permute-start.11 = (f32[8,3072]{1,0:T(8,128)S(1)}, f32[8,3072]{1,0:T(8,128)S(1)}, u32[]{:S(2)}, u32[]{:S(2)}) collective-permute-start(f32[8,3072]{1,0:T(8,128)S(1)} %fusion.2), channel_id=1, source_target_pairs={{0,2},{1,3},{2,4},{3,5},{4,6},{5,7},{6,8},{7,9},{8,10},{9,11},{10,... | collective-permute-start | bytes 294920
  448.3 10.2 %collective-permute-start.12 = (f32[8,3072]{1,0:T(8,128)S(1)}, f32[8,3072]{1,0:T(8,128)}, u32[]{:S(2)}, u32[]{:S(2)}) collective-permute-start(f32[8,3072]{1,0:T(8,128)S(1)} %fusion.2), channel_id=1, source_target_pairs={{0,3},{1,4},{2,5},{3,6},{4,7},{5,8},{6,9},{7,10},{8,11},{9,12},{10... | collective-permute-start | bytes 294920
  452.9 4.9 %collective-permute-start.13 = (f32[6,3072]{1,0:T(8,128)S(1)}, f32[6,3072]{1,0:T(8,128)S(1)}, u32[]{:S(2)}, u32[]{:S(2)}) collective-permute-start(f32[6,3072]{1,0:T(8,128)S(1)} %slice.38), channel_id=1, source_target_pairs={{0,4},{1,5},{2,6},{3,7},{4,8},{5,9},{6,10},{7,11},{8,12},{9,13},{1... | collective-permute-start | bytes 221192
  457.8 0.6 copy-start.5
where the time goes:
time: 464 us; the launch traced here: 462 us
  blocking collectives  293 us (63%)
  starting transfers between devices  63.1 us (14%)
  matrix products  61.8 us (13%)
  local copies, waits for them, and re-layouts  27.9 us (6%)
  waiting for transfers between devices  9.39 us (2%)
  other arithmetic  5.04 us (1%)
    unnamed x3, blocking collectives  149 us
    all_gather x3, blocking collectives, on_device(): all_normed = lax.all_gather(normed, 'ep', axis=0, tiled=True)  145 us
    unnamed x12, starting transfers between devices  31.3 us
    dot_general x6, matrix products, gated_block(): return jnp.dot(hidden, w_down, preferred_element_type=jnp.float32)  23.4 us
    dot_general x6, matrix products, gated_block(): gate_part = jnp.dot(inputs, w_gate, preferred_element_type=jnp.float32)  20.6 us
    all_to_all x3, starting transfers between devices, on_device(): lax.all_to_all(outgoing, 'ep', split_axis=0, concat_axis=0, tiled=True)  18.3 us
    unnamed x38, local copies, waits for them, and re-layouts  12.9 us
    all_to_all x3, starting transfers between devices, on_device(): lax.all_to_all(produced, 'ep', split_axis=0, concat_axis=0, tiled=True)  10.8 us
  transfers between devices with their start and end apart: 20, of which 7 were waited for; matrix products, arithmetic and copies ran while one was open for 6% of the time, Pallas kernels for 0%

commit v1 on v0

--- a/solution.py
+++ b/solution.py
@@ -78,7 +78,19 @@
         route_rows = lax.dynamic_index_in_dim(route_ids[0], micro_index, 0, keepdims=False)
         widened, normed = normalize(current, gain)
         weights, picked, zero_share = choice_weights(normed, route_rows, router_w, n_groups)
-        all_normed = lax.all_gather(normed, "ep", axis=0, tiled=True)
+
+        def match_masks(base_x, dim_no):
+            return jnp.concatenate(
+                lax.all_to_all(
+                    jnp.stack(lax.psum(1, axis_name="ep") * [base_x]),
+                    "ep",
+                    split_axis=0,
+                    concat_axis=0,
+                ),
+                axis=dim_no,
+            )
+
+        all_normed = match_masks(normed, 0)
         real_pick = picked[:, :, :n_groups]
         hot = jnp.sum(real_pick, axis=1)
         coef = jnp.einsum("tk,tke->te", weights, real_pick, precision=lax.Precision.HIGHEST)

time: 464 us -> 396 us (0.85)
  blocking collectives: 293 us -> 148 us
  waiting for transfers between devices: 9.39 us -> 53.1 us
  starting transfers between devices: 63.1 us -> 81.5 us
  local copies, waits for them, and re-layouts: 27.9 us -> 37.5 us
    all_gather x3 -> x0, blocking collectives: 145 us -> none  [on_device(): all_normed = lax.all_gather(normed, 'ep', axis=0, tiled=True)]
    all_to_all x3, waiting for transfers between devices: 0.01 us -> 22 us  [on_device(): lax.all_to_all(outgoing, 'ep', split_axis=0, concat_axis=0, tiled=True)]
    all_to_all x0 -> x3, waiting for transfers between devices: none -> 17.9 us  [match_masks(): lax.all_to_all(jnp.stack(lax.psum(1, axis_name='ep') * [base_x]), 'ep', s...]
    all_to_all x0 -> x3, starting transfers between devices: none -> 11 us  [match_masks(): lax.all_to_all(jnp.stack(lax.psum(1, axis_name='ep') * [base_x]), 'ep', s...]
    all_to_all x3, waiting for transfers between devices: 2.82 us -> 8.1 us  [on_device(): lax.all_to_all(produced, 'ep', split_axis=0, concat_axis=0, tiled=True)]
    unnamed x38 -> x95, local copies, waits for them, and re-layouts: 12.9 us -> 13.1 us
  transfers between devices with their start and end apart: 20 -> 23, of which waited for: 7 -> 13; matrix products, arithmetic and copies ran while one was open for 6% -> 18% of each run, Pallas kernels for 0% -> 0%
where the time goes in v1:
time: 396 us; the launch traced here: 392 us
  blocking collectives  148 us (37%)
  starting transfers between devices  81.5 us (21%)
  matrix products  60.3 us (15%)
  waiting for transfers between devices  53.1 us (13%)
  local copies, waits for them, and re-layouts  37.5 us (9%)
  other arithmetic  9.59 us (2%)
    unnamed x3, blocking collectives  148 us
    unnamed x12, starting transfers between devices  30.6 us
    dot_general x6, matrix products, gated_block(): return jnp.dot(hidden, w_down, preferred_element_type=jnp.float32)  23.6 us
    all_to_all x3, starting transfers between devices, on_device(): lax.all_to_all(outgoing, 'ep', split_axis=0, concat_axis=0, tiled=True)  22.3 us
    all_to_all x3, waiting for transfers between devices, on_device(): lax.all_to_all(outgoing, 'ep', split_axis=0, concat_axis=0, tiled=True)  22 us
    dot_general x6, matrix products, gated_block(): gate_part = jnp.dot(inputs, w_gate, preferred_element_type=jnp.float32)  18.6 us
    all_to_all x3, waiting for transfers between devices, match_masks(): lax.all_to_all(jnp.stack(lax.psum(1, axis_name='ep') * [base_x]), 'ep', s...  17.9 us
    all_to_all x3, starting transfers between devices, on_device(): lax.all_to_all(produced, 'ep', split_axis=0, concat_axis=0, tiled=True)  14.9 us
  transfers between devices with their start and end apart: 23, of which 13 were waited for; matrix products, arithmetic and copies ran while one was open for 18% of the time, Pallas kernels for 0%

profile of v1, /device:TPU:0, one launch (start us, length us, event | category | flops | bytes accessed | tf_op | source)
XLA Modules:
  0.0 392.0 jit_solution(9857709186479803796)
XLA Ops:
  1.5 1.7 fusion.196
  5.3 8.3 %all-to-all-start.1 = ((bf16[16,2,3072]{2,1,0:T(2,128)(2,1)}), bf16[16,2,3072]{2,1,0:T(2,128)(2,1)S(1)}, u32[]{:S(2)}, u32[]{:S(2)}) async-start(bf16[16,2,3072]{2,1,0:T(2,128)(2,1)} %copy.46), calls=%async_computation.1 | async-start | bytes 393216 | tf_op jit(solution)/shard_map/all_to_all | solution.py:104
  15.3 7.0 %all-to-all-done.1 = bf16[16,2,3072]{2,1,0:T(2,128)(2,1)S(1)} async-done(((bf16[16,2,3072]{2,1,0:T(2,128)(2,1)}), bf16[16,2,3072]{2,1,0:T(2,128)(2,1)S(1)}, u32[]{:S(2)}, u32[]{:S(2)}) %all-to-all-start.1) | async-done | bytes 196640 | tf_op jit(solution)/shard_map/all_to_all | solution.py:104
  23.2 3.6 all-to-all-start
  27.9 4.1 %fusion.19 = f32[32,1024]{1,0:T(8,128)S(1)} fusion(bf16[32,3072]{1,0:T(8,128)(2,1)S(1)} %reshape.117, bf16[1,1,3072,1024]{3,2,1,0:T(8,128)(2,1)} %param.17), kind=kOutput, calls=%fused_computation.16 | convolution fusion | flops 201326592 | bytes 6619136 | tf_op jit(solution)/shard_map/dot_general | solution.py:21
  33.8 4.0 %fusion.7 = f32[16,2,3072]{2,0,1:T(8,128)S(1)} fusion(bf16[1,1,1024,3072]{3,2,1,0:T(8,128)(2,1)} %param.19, bf16[16,2,1024]{2,1,0:T(2,128)(2,1)S(1)} %dot_general.111), kind=kOutput, calls=%fused_computation.4 | convolution fusion | flops 201326592 | bytes 6750208 | tf_op jit(solution)/shard_map/dot_general | solution.py:24
  38.8 7.1 %all-to-all-done = bf16[16,6,3072]{2,1,0:T(8,128)(2,1)S(1)} async-done(((bf16[16,6,3072]{2,1,0:T(8,128)(2,1)}), bf16[16,6,3072]{2,1,0:T(8,128)(2,1)S(1)}, u32[]{:S(2)}, u32[]{:S(2)}) %all-to-all-start) | async-done | bytes 589856 | tf_op jit(solution)/shard_map/all_to_all | solution.py:84
  45.9 5.0 %all-to-all-start.2 = ((f32[16,2,3072]{2,1,0:T(2,128)}), f32[16,2,3072]{2,1,0:T(2,128)}, u32[]{:S(2)}, u32[]{:S(2)}) async-start(f32[16,2,3072]{2,1,0:T(2,128)} %copy.48), calls=%async_computation.2 | async-start | bytes 786432 | tf_op jit(solution)/shard_map/all_to_all | solution.py:107
  52.4 1.3 reshape.116
  53.8 2.2 fusion.40
  56.0 3.9 fusion.28
  59.9 2.7 all-to-all-done.2
  62.6 1.5 fusion.23
  64.0 1.7 add.116
  65.7 49.3 %fusion = f32[8,3072]{1,0:T(8,128)S(1)} fusion(f32[96,3072]{1,0:T(8,128)} %add.116), kind=kCustom, calls=%all-reduce-scatter | all-reduce-scatter fusion | flops 393217 | bytes 1278464
  115.1 3.6 collective-permute-start.2
  118.6 1.3 collective-permute-start.3
  119.9 1.9 collective-permute-start.4
  121.9 3.6 collective-permute-start.5
  125.7 2.1 collective-permute-done.5
  129.0 3.3 concatenate
  135.9 6.4 %all-to-all-start.4 = ((bf16[16,2,3072]{2,1,0:T(2,128)(2,1)}), bf16[16,2,3072]{2,1,0:T(2,128)(2,1)S(1)}, u32[]{:S(2)}, u32[]{:S(2)}) async-start(bf16[16,2,3072]{2,1,0:T(2,128)(2,1)} %copy.52), calls=%async_computation.4 | async-start | bytes 393216 | tf_op jit(solution)/shard_map/all_to_all | solution.py:104
  143.4 8.1 %all-to-all-done.4 = bf16[16,2,3072]{2,1,0:T(2,128)(2,1)S(1)} async-done(((bf16[16,2,3072]{2,1,0:T(2,128)(2,1)}), bf16[16,2,3072]{2,1,0:T(2,128)(2,1)S(1)}, u32[]{:S(2)}, u32[]{:S(2)}) %all-to-all-start.4) | async-done | bytes 196640 | tf_op jit(solution)/shard_map/all_to_all | solution.py:104
  152.5 3.8 all-to-all-start.3
  157.3 4.0 %fusion.17 = f32[32,1024]{1,0:T(8,128)S(1)} fusion(bf16[32,3072]{1,0:T(8,128)(2,1)S(1)} %reshape.119, bf16[1,1,3072,1024]{3,2,1,0:T(8,128)(2,1)} %param.17), kind=kOutput, calls=%fused_computation.14 | convolution fusion | flops 201326592 | bytes 6619136 | tf_op jit(solution)/shard_map/dot_general | solution.py:21
  161.3 4.0 %fusion.72 = bf16[32,1024]{1,0:T(8,128)(2,1)S(1)} fusion(bf16[32,3072]{1,0:T(8,128)(2,1)S(1)} %reshape.119, bf16[1,1,3072,1024]{3,2,1,0:T(8,128)(2,1)} %param.18, f32[32,1024]{1,0:T(8,128)S(1)} %fusion.17), kind=kOutput, calls=%fused_computation.55 | convolution fusion | flops 201523200 | bytes 6684672 | tf_op jit(solution)/shard_map/dot_general | solution.py:22
  165.3 4.0 %fusion.5 = f32[16,2,3072]{2,0,1:T(8,128)S(1)} fusion(bf16[1,1,1024,3072]{3,2,1,0:T(8,128)(2,1)} %param.19, bf16[16,2,1024]{2,1,0:T(2,128)(2,1)S(1)} %dot_general.123), kind=kOutput, calls=%fused_computation.2 | convolution fusion | flops 201326592 | bytes 6750208 | tf_op jit(solution)/shard_map/dot_general | solution.py:24
  170.3 4.8 %all-to-all-done.3 = bf16[16,6,3072]{2,1,0:T(8,128)(2,1)S(1)} async-done(((bf16[16,6,3072]{2,1,0:T(8,128)(2,1)}), bf16[16,6,3072]{2,1,0:T(8,128)(2,1)S(1)}, u32[]{:S(2)}, u32[]{:S(2)}) %all-to-all-start.3) | async-done | bytes 589856 | tf_op jit(solution)/shard_map/all_to_all | solution.py:84
  175.2 5.0 %all-to-all-start.5 = ((f32[16,2,3072]{2,1,0:T(2,128)}), f32[16,2,3072]{2,1,0:T(2,128)S(1)}, u32[]{:S(2)}, u32[]{:S(2)}) async-start(f32[16,2,3072]{2,1,0:T(2,128)} %copy.54), calls=%async_computation.5 | async-start | bytes 786432 | tf_op jit(solution)/shard_map/all_to_all | solution.py:107
  181.6 1.3 reshape.118
  182.9 2.2 fusion.38
  185.1 3.9 fusion.26
  189.0 2.8 all-to-all-done.5
  191.8 1.3 fusion.22
  193.1 1.7 add.123
  194.8 49.5 %fusion.1 = f32[8,3072]{1,0:T(8,128)S(1)} fusion(f32[96,3072]{1,0:T(8,128)} %add.123), kind=kCustom, calls=%all-reduce-scatter.1 | all-reduce-scatter fusion | flops 393217 | bytes 1278464
  244.3 3.1 collective-permute-start.6
  247.5 1.3 collective-permute-start.7
  248.8 1.9 collective-permute-start.8
  250.7 3.6 collective-permute-start.9
  255.1 1.4 collective-permute-done.9
  257.1 2.4 concatenate.1
  265.9 7.6 %all-to-all-start.7 = ((bf16[16,2,3072]{2,1,0:T(2,128)(2,1)}), bf16[16,2,3072]{2,1,0:T(2,128)(2,1)S(1)}, u32[]{:S(2)}, u32[]{:S(2)}) async-start(bf16[16,2,3072]{2,1,0:T(2,128)(2,1)} %copy.57), calls=%async_computation.7 | async-start | bytes 393216 | tf_op jit(solution)/shard_map/all_to_all | solution.py:104
  273.8 1.4 select_reduce_fusion
  275.2 6.9 %all-to-all-done.7 = bf16[16,2,3072]{2,1,0:T(2,128)(2,1)S(1)} async-done(((bf16[16,2,3072]{2,1,0:T(2,128)(2,1)}), bf16[16,2,3072]{2,1,0:T(2,128)(2,1)S(1)}, u32[]{:S(2)}, u32[]{:S(2)}) %all-to-all-start.7) | async-done | bytes 196640 | tf_op jit(solution)/shard_map/all_to_all | solution.py:104
  283.1 3.6 all-to-all-start.6
  286.9 4.0 %fusion.15 = f32[32,1024]{1,0:T(8,128)S(1)} fusion(bf16[32,3072]{1,0:T(8,128)(2,1)S(1)} %reshape.121, bf16[1,1,3072,1024]{3,2,1,0:T(8,128)(2,1)} %param.17), kind=kOutput, calls=%fused_computation.12 | convolution fusion | flops 201326592 | bytes 6619136 | tf_op jit(solution)/shard_map/dot_general | solution.py:21
  290.8 4.0 %fusion.69 = bf16[32,1024]{1,0:T(8,128)(2,1)S(1)} fusion(bf16[32,3072]{1,0:T(8,128)(2,1)S(1)} %reshape.121, bf16[1,1,3072,1024]{3,2,1,0:T(8,128)(2,1)} %param.18, f32[32,1024]{1,0:T(8,128)S(1)} %fusion.15), kind=kOutput, calls=%fused_computation.54 | convolution fusion | flops 201523200 | bytes 6684672 | tf_op jit(solution)/shard_map/dot_general | solution.py:22
  294.8 4.0 %fusion.3 = f32[16,2,3072]{2,0,1:T(8,128)S(1)} fusion(bf16[1,1,1024,3072]{3,2,1,0:T(8,128)(2,1)} %param.19, bf16[16,2,1024]{2,1,0:T(2,128)(2,1)S(1)} %dot_general.135), kind=kOutput, calls=%fused_computation | convolution fusion | flops 201326592 | bytes 6750208 | tf_op jit(solution)/shard_map/dot_general | solution.py:24
  299.9 6.0 %all-to-all-done.6 = bf16[16,6,3072]{2,1,0:T(8,128)(2,1)S(1)} async-done(((bf16[16,6,3072]{2,1,0:T(8,128)(2,1)}), bf16[16,6,3072]{2,1,0:T(8,128)(2,1)S(1)}, u32[]{:S(2)}, u32[]{:S(2)}) %all-to-all-start.6) | async-done | bytes 589856 | tf_op jit(solution)/shard_map/all_to_all | solution.py:84
  305.8 5.0 %all-to-all-start.8 = ((f32[16,2,3072]{2,1,0:T(2,128)}), f32[16,2,3072]{2,1,0:T(2,128)S(1)}, u32[]{:S(2)}, u32[]{:S(2)}) async-start(f32[16,2,3072]{2,1,0:T(2,128)} %copy.59), calls=%async_computation.8 | async-start | bytes 786432 | tf_op jit(solution)/shard_map/all_to_all | solution.py:107
  312.3 1.3 reshape.120
  313.6 2.2 fusion.36
  315.8 3.9 fusion.24
  319.7 2.7 all-to-all-done.8
  322.4 1.3 fusion.21
  323.7 1.7 add.130
  325.4 49.6 %fusion.2 = f32[8,3072]{1,0:T(8,128)S(1)} fusion(f32[96,3072]{1,0:T(8,128)} %add.130), kind=kCustom, calls=%all-reduce-scatter.2 | all-reduce-scatter fusion | flops 393217 | bytes 1278464
  375.0 3.5 collective-permute-start.10
  378.5 1.3 collective-permute-start.11
  379.8 1.9 collective-permute-start.12
  381.7 3.5 collective-permute-start.13
  386.0 1.4 collective-permute-done.13
  388.1 2.4 concatenate.2
  (167 shorter events, 35.7 us)
Async XLA Ops:
  0.0 56.0 %copy-start = (bf16[1,384,3072]{2,1,0:T(8,128)(2,1)S(1)}, bf16[1,384,3072]{2,1,0:T(8,128)(2,1)}, u32[]{:S(2)}) copy-start(bf16[1,384,3072]{2,1,0:T(8,128)(2,1)} %param.16) | copy-start | bytes 7077892
  0.9 27.0 %copy-start.28 = (s32[1,1,6,8]{3,1,2,0:T(1,128)}, s32[1,1,6,8]{3,1,2,0:T(1,128)S(1)}, u32[]{:S(2)}) copy-start(s32[1,1,6,8]{3,1,2,0:T(1,128)S(1)} %get-tuple-element.15) | copy-start | bytes 580
  0.9 27.0 %copy-start.29 = (s32[1,1,6,8]{3,1,2,0:T(1,128)}, s32[1,1,6,8]{3,1,2,0:T(1,128)S(1)}, u32[]{:S(2)}) copy-start(s32[1,1,6,8]{3,1,2,0:T(1,128)S(1)} %get-tuple-element.16) | copy-start | bytes 580
  3.4 10.3 %copy-start.38 = (f32[6]{0:T(128)}, f32[6]{0:T(128)S(1)}, u32[]{:S(2)}) copy-start(f32[6]{0:T(128)S(1)} %add_rsqrt_fusion.2) | copy-start | bytes 76
  5.3 17.0 %all-to-all-start.1 = ((bf16[16,2,3072]{2,1,0:T(2,128)(2,1)}), bf16[16,2,3072]{2,1,0:T(2,128)(2,1)S(1)}, u32[]{:S(2)}, u32[]{:S(2)}) async-start(bf16[16,2,3072]{2,1,0:T(2,128)(2,1)} %copy.46), calls=%async_computation.1 | async-start | bytes 393216 | tf_op jit(solution)/shard_map/all_to_all | solution.py:104
  14.9 17.1 %copy-start.36 = (f32[6,8]{1,0:T(8,128)}, f32[6,8]{1,0:T(8,128)S(1)}, u32[]{:S(2)}) copy-start(f32[6,8]{1,0:T(8,128)S(1)} %select_reduce_fusion.2) | copy-start | bytes 580
  15.0 36.0 %copy-start.27 = (s32[6,8]{1,0:T(8,128)}, s32[6,8]{1,0:T(8,128)S(1)}, u32[]{:S(2)}) copy-start(s32[6,8]{1,0:T(8,128)S(1)} %get-tuple-element.18) | copy-start | bytes 580
  15.1 12.8 %copy-start.33 = (pred[6,8,24]{2,1,0:T(8,128)(4,1)}, pred[6,8,24]{2,1,0:T(8,128)(4,1)S(1)}, u32[]{:S(2)}) copy-start(pred[6,8,24]{2,1,0:T(8,128)(4,1)S(1)} %iota_compare_fusion.1) | copy-start | bytes 3460
  15.2 119.5 %copy-start.25 = (f32[16,6]{0,1:T(8,128)}, f32[16,6]{0,1:T(8,128)S(1)}, u32[]{:S(2)}) copy-start(f32[16,6]{0,1:T(8,128)S(1)} %bitcast_subtract_fusion.1) | copy-start | bytes 1156
  22.3 1.0 copy-start.13
  23.2 22.7 %all-to-all-start = ((bf16[16,6,3072]{2,1,0:T(8,128)(2,1)}), bf16[16,6,3072]{2,1,0:T(8,128)(2,1)S(1)}, u32[]{:S(2)}, u32[]{:S(2)}) async-start(bf16[16,6,3072]{2,1,0:T(8,128)(2,1)} %stack.9), calls=%async_computation | async-start | bytes 1572864 | tf_op jit(solution)/shard_map/all_to_all | solution.py:84
  27.9 4.6 %copy-start.1 = (bf16[1,1,3072,1024]{3,2,1,0:T(8,128)(2,1)S(1)}, bf16[1,1,3072,1024]{3,2,1,0:T(8,128)(2,1)}, u32[]{:S(2)}) copy-start(bf16[1,1,3072,1024]{3,2,1,0:T(8,128)(2,1)} %param.18) | copy-start | bytes 18874372
  33.7 17.3 %copy-start.42 = (u32[32]{0:T(128)S(1)}, u32[32]{0:T(128)}, u32[]{:S(2)}) copy-start(u32[32]{0:T(128)} %constant.91) | copy-start | bytes 388
  45.9 6.5 %copy-start.2 = (bf16[16,6,3072]{2,1,0:T(8,128)(2,1)}, bf16[16,6,3072]{2,1,0:T(8,128)(2,1)S(1)}, u32[]{:S(2)}) copy-start(bf16[16,6,3072]{2,1,0:T(8,128)(2,1)S(1)} %all-to-all-done) | copy-start | bytes 1769476
  45.9 16.6 %all-to-all-start.2 = ((f32[16,2,3072]{2,1,0:T(2,128)}), f32[16,2,3072]{2,1,0:T(2,128)}, u32[]{:S(2)}, u32[]{:S(2)}) async-start(f32[16,2,3072]{2,1,0:T(2,128)} %copy.48), calls=%async_computation.2 | async-start | bytes 786432 | tf_op jit(solution)/shard_map/all_to_all | solution.py:107
  51.0 82.7 %copy-start.32 = (pred[6,8,24]{2,1,0:T(8,128)(4,1)}, pred[6,8,24]{2,1,0:T(8,128)(4,1)S(1)}, u32[]{:S(2)}) copy-start(pred[6,8,24]{2,1,0:T(8,128)(4,1)S(1)} %iota_compare_fusion) | copy-start | bytes 3460
  56.0 69.6 %copy-start.31 = (s32[1,1,6,8]{3,1,2,0:T(1,128)S(1)}, s32[1,1,6,8]{3,1,2,0:T(1,128)}, u32[]{:S(2)}) copy-start(s32[1,1,6,8]{3,1,2,0:T(1,128)} %copy-done.30) | copy-start | bytes 580
  56.0 69.6 %copy-start.37 = (f32[6,8]{1,0:T(8,128)S(1)}, f32[6,8]{1,0:T(8,128)}, u32[]{:S(2)}) copy-start(f32[6,8]{1,0:T(8,128)} %copy-done.36) | copy-start | bytes 580
  59.9 72.4 %copy-start.39 = (f32[6]{0:T(128)S(1)}, f32[6]{0:T(128)}, u32[]{:S(2)}) copy-start(f32[6]{0:T(128)} %copy-done.38) | copy-start | bytes 76
  59.9 74.7 %copy-start.15 = (bf16[1,6,3072]{2,0,1:T(2,128)(2,1)S(1)}, bf16[1,6,3072]{2,0,1:T(2,128)(2,1)}, u32[]{:S(2)}) copy-start(bf16[1,6,3072]{2,0,1:T(2,128)(2,1)} %get-tuple-element.13) | copy-start | bytes 110596
  64.0 78.4 %copy-start.17 = (bf16[1,3072,24]{1,2,0:T(8,128)(2,1)S(1)}, bf16[1,3072,24]{1,2,0:T(8,128)(2,1)}, u32[]{:S(2)}) copy-start(bf16[1,3072,24]{1,2,0:T(8,128)(2,1)} %param.13) | copy-start | bytes 442372
  115.1 12.6 %collective-permute-start.2 = (f32[8,3072]{1,0:T(8,128)S(1)}, f32[8,3072]{1,0:T(8,128)S(1)}, u32[]{:S(2)}, u32[]{:S(2)}) collective-permute-start(f32[8,3072]{1,0:T(8,128)S(1)} %fusion), channel_id=1, source_target_pairs={{0,1},{1,2},{2,3},{3,4},{4,5},{5,6},{6,7},{7,8},{8,9},{9,10},{10,1... | collective-permute-start | bytes 294920
  118.6 9.1 %collective-permute-start.3 = (f32[8,3072]{1,0:T(8,128)S(1)}, f32[8,3072]{1,0:T(8,128)S(1)}, u32[]{:S(2)}, u32[]{:S(2)}) collective-permute-start(f32[8,3072]{1,0:T(8,128)S(1)} %fusion), channel_id=1, source_target_pairs={{0,2},{1,3},{2,4},{3,5},{4,6},{5,7},{6,8},{7,9},{8,10},{9,11},{10,... | collective-permute-start | bytes 294920
  119.9 9.1 %collective-permute-start.4 = (f32[8,3072]{1,0:T(8,128)S(1)}, f32[8,3072]{1,0:T(8,128)}, u32[]{:S(2)}, u32[]{:S(2)}) collective-permute-start(f32[8,3072]{1,0:T(8,128)S(1)} %fusion), channel_id=1, source_target_pairs={{0,3},{1,4},{2,5},{3,6},{4,7},{5,8},{6,9},{7,10},{8,11},{9,12},{10... | collective-permute-start | bytes 294920
  121.9 5.8 %collective-permute-start.5 = (f32[6,3072]{1,0:T(8,128)S(1)}, f32[6,3072]{1,0:T(8,128)S(1)}, u32[]{:S(2)}, u32[]{:S(2)}) collective-permute-start(f32[6,3072]{1,0:T(8,128)S(1)} %slice.36), channel_id=1, source_target_pairs={{0,4},{1,5},{2,6},{3,7},{4,8},{5,9},{6,10},{7,11},{8,12},{9,13},{1... | collective-permute-start | bytes 221192
  127.7 0.6 copy-start.22
  132.4 28.8 %copy-start.5 = (bf16[2,6,3072]{2,1,0:T(8,128)(2,1)}, bf16[2,6,3072]{2,1,0:T(8,128)(2,1)S(1)}, u32[]{:S(2)}) copy-start(bf16[2,6,3072]{2,1,0:T(8,128)(2,1)S(1)} %get-tuple-element.11) | copy-start | bytes 221188
  132.4 2.2 collective-permute-start
  133.8 27.5 %copy-start.19 = (f32[6,16]{1,0:T(8,128)}, f32[6,16]{1,0:T(8,128)S(1)}, u32[]{:S(2)}) copy-start(f32[6,16]{1,0:T(8,128)S(1)} %convert_reduce_fusion) | copy-start | bytes 1156
  134.7 17.7 %copy-start.11 = (bf16[6,3072]{1,0:T(8,128)(2,1)}, bf16[6,3072]{1,0:T(8,128)(2,1)S(1)}, u32[]{:S(2)}) copy-start(bf16[6,3072]{1,0:T(8,128)(2,1)S(1)} %get-tuple-element.10) | copy-start | bytes 110596
  134.8 26.5 %copy-start.41 = (f32[6]{0:T(128)}, f32[6]{0:T(128)S(1)}, u32[]{:S(2)}) copy-start(f32[6]{0:T(128)S(1)} %add_rsqrt_fusion.1) | copy-start | bytes 76
  135.9 15.6 %all-to-all-start.4 = ((bf16[16,2,3072]{2,1,0:T(2,128)(2,1)}), bf16[16,2,3072]{2,1,0:T(2,128)(2,1)S(1)}, u32[]{:S(2)}, u32[]{:S(2)}) async-start(bf16[16,2,3072]{2,1,0:T(2,128)(2,1)} %copy.52), calls=%async_computation.4 | async-start | bytes 393216 | tf_op jit(solution)/shard_map/all_to_all | solution.py:104
  151.5 1.0 copy-start.14
  152.5 22.7 %all-to-all-start.3 = ((bf16[16,6,3072]{2,1,0:T(8,128)(2,1)}), bf16[16,6,3072]{2,1,0:T(8,128)(2,1)S(1)}, u32[]{:S(2)}, u32[]{:S(2)}) async-start(bf16[16,6,3072]{2,1,0:T(8,128)(2,1)} %stack.10), calls=%async_computation.3 | async-start | bytes 1572864 | tf_op jit(solution)/shard_map/all_to_all | solution.py:84
  175.2 5.8 %copy-start.3 = (bf16[16,6,3072]{2,1,0:T(8,128)(2,1)}, bf16[16,6,3072]{2,1,0:T(8,128)(2,1)S(1)}, u32[]{:S(2)}) copy-start(bf16[16,6,3072]{2,1,0:T(8,128)(2,1)S(1)} %all-to-all-done.3) | copy-start | bytes 1769476
  175.2 16.6 %all-to-all-start.5 = ((f32[16,2,3072]{2,1,0:T(2,128)}), f32[16,2,3072]{2,1,0:T(2,128)S(1)}, u32[]{:S(2)}, u32[]{:S(2)}) async-start(f32[16,2,3072]{2,1,0:T(2,128)} %copy.54), calls=%async_computation.5 | async-start | bytes 786432 | tf_op jit(solution)/shard_map/all_to_all | solution.py:107
  185.1 6.7 %copy-start.26 = (f32[16,6]{0,1:T(8,128)S(1)}, f32[16,6]{0,1:T(8,128)}, u32[]{:S(2)}) copy-start(f32[16,6]{0,1:T(8,128)} %copy-done.25) | copy-start | bytes 1156
  185.1 6.7 %copy-start.34 = (f32[6,1,16]{2,0,1:T(8,128)S(1)}, f32[6,1,16]{2,0,1:T(8,128)}, u32[]{:S(2)}) copy-start(f32[6,1,16]{2,0,1:T(8,128)} %copy.123) | copy-start | bytes 1156
  189.0 70.5 %copy-start.6 = (bf16[2,6,3072]{2,1,0:T(8,128)(2,1)S(1)}, bf16[2,6,3072]{2,1,0:T(8,128)(2,1)}, u32[]{:S(2)}) copy-start(bf16[2,6,3072]{2,1,0:T(8,128)(2,1)} %copy-done.5) | copy-start | bytes 221188
  189.0 70.5 %copy-start.12 = (bf16[6,3072]{1,0:T(8,128)(2,1)S(1)}, bf16[6,3072]{1,0:T(8,128)(2,1)}, u32[]{:S(2)}) copy-start(bf16[6,3072]{1,0:T(8,128)(2,1)} %copy-done.11) | copy-start | bytes 110596
  193.1 80.4 %copy-start.18 = (bf16[1,3072,24]{1,2,0:T(8,128)(2,1)S(1)}, bf16[1,3072,24]{1,2,0:T(8,128)(2,1)}, u32[]{:S(2)}) copy-start(bf16[1,3072,24]{1,2,0:T(8,128)(2,1)} %param.13) | copy-start | bytes 442372
  244.3 12.2 %collective-permute-start.6 = (f32[8,3072]{1,0:T(8,128)S(1)}, f32[8,3072]{1,0:T(8,128)S(1)}, u32[]{:S(2)}, u32[]{:S(2)}) collective-permute-start(f32[8,3072]{1,0:T(8,128)S(1)} %fusion.1), channel_id=1, source_target_pairs={{0,1},{1,2},{2,3},{3,4},{4,5},{5,6},{6,7},{7,8},{8,9},{9,10},{10,1... | collective-permute-start | bytes 294920
  247.5 9.0 %collective-permute-start.7 = (f32[8,3072]{1,0:T(8,128)S(1)}, f32[8,3072]{1,0:T(8,128)S(1)}, u32[]{:S(2)}, u32[]{:S(2)}) collective-permute-start(f32[8,3072]{1,0:T(8,128)S(1)} %fusion.1), channel_id=1, source_target_pairs={{0,2},{1,3},{2,4},{3,5},{4,6},{5,7},{6,8},{7,9},{8,10},{9,11},{10,... | collective-permute-start | bytes 294920
  248.8 8.4 %collective-permute-start.8 = (f32[8,3072]{1,0:T(8,128)S(1)}, f32[8,3072]{1,0:T(8,128)}, u32[]{:S(2)}, u32[]{:S(2)}) collective-permute-start(f32[8,3072]{1,0:T(8,128)S(1)} %fusion.1), channel_id=1, source_target_pairs={{0,3},{1,4},{2,5},{3,6},{4,7},{5,8},{6,9},{7,10},{8,11},{9,12},{10... | collective-permute-start | bytes 294920
  250.7 5.8 %collective-permute-start.9 = (f32[6,3072]{1,0:T(8,128)S(1)}, f32[6,3072]{1,0:T(8,128)S(1)}, u32[]{:S(2)}, u32[]{:S(2)}) collective-permute-start(f32[6,3072]{1,0:T(8,128)S(1)} %slice.37), channel_id=1, source_target_pairs={{0,4},{1,5},{2,6},{3,7},{4,8},{5,9},{6,10},{7,11},{8,12},{9,13},{1... | collective-permute-start | bytes 221192
  256.5 0.6 copy-start.23
  260.4 22.8 %copy-start.7 = (bf16[2,6,3072]{2,1,0:T(8,128)(2,1)}, bf16[2,6,3072]{2,1,0:T(8,128)(2,1)S(1)}, u32[]{:S(2)}) copy-start(bf16[2,6,3072]{2,1,0:T(8,128)(2,1)S(1)} %get-tuple-element.7) | copy-start | bytes 221188
  260.4 2.6 collective-permute-start.1
  264.0 19.1 %copy-start.9 = (bf16[6,3072]{1,0:T(8,128)(2,1)}, bf16[6,3072]{1,0:T(8,128)(2,1)S(1)}, u32[]{:S(2)}) copy-start(bf16[6,3072]{1,0:T(8,128)(2,1)S(1)} %get-tuple-element.6) | copy-start | bytes 110596
  264.1 19.1 %copy-start.40 = (f32[6]{0:T(128)}, f32[6]{0:T(128)S(1)}, u32[]{:S(2)}) copy-start(f32[6]{0:T(128)S(1)} %add_rsqrt_fusion) | copy-start | bytes 76
  265.9 16.2 %all-to-all-start.7 = ((bf16[16,2,3072]{2,1,0:T(2,128)(2,1)}), bf16[16,2,3072]{2,1,0:T(2,128)(2,1)S(1)}, u32[]{:S(2)}, u32[]{:S(2)}) async-start(bf16[16,2,3072]{2,1,0:T(2,128)(2,1)} %copy.57), calls=%async_computation.7 | async-start | bytes 393216 | tf_op jit(solution)/shard_map/all_to_all | solution.py:104
  283.1 22.7 %all-to-all-start.6 = ((bf16[16,6,3072]{2,1,0:T(8,128)(2,1)}), bf16[16,6,3072]{2,1,0:T(8,128)(2,1)S(1)}, u32[]{:S(2)}, u32[]{:S(2)}) async-start(bf16[16,6,3072]{2,1,0:T(8,128)(2,1)} %stack.11), calls=%async_computation.6 | async-start | bytes 1572864 | tf_op jit(solution)/shard_map/all_to_all | solution.py:84
  305.8 5.8 %copy-start.4 = (bf16[16,6,3072]{2,1,0:T(8,128)(2,1)}, bf16[16,6,3072]{2,1,0:T(8,128)(2,1)S(1)}, u32[]{:S(2)}) copy-start(bf16[16,6,3072]{2,1,0:T(8,128)(2,1)S(1)} %all-to-all-done.6) | copy-start | bytes 1769476
  305.8 16.5 %all-to-all-start.8 = ((f32[16,2,3072]{2,1,0:T(2,128)}), f32[16,2,3072]{2,1,0:T(2,128)S(1)}, u32[]{:S(2)}, u32[]{:S(2)}) async-start(f32[16,2,3072]{2,1,0:T(2,128)} %copy.59), calls=%async_computation.8 | async-start | bytes 786432 | tf_op jit(solution)/shard_map/all_to_all | solution.py:107
  315.8 6.6 %copy-start.20 = (f32[6,16]{1,0:T(8,128)S(1)}, f32[6,16]{1,0:T(8,128)}, u32[]{:S(2)}) copy-start(f32[6,16]{1,0:T(8,128)} %copy-done.19) | copy-start | bytes 1156
  315.8 6.6 %copy-start.35 = (f32[6,1,16]{2,0,1:T(8,128)S(1)}, f32[6,1,16]{2,0,1:T(8,128)}, u32[]{:S(2)}) copy-start(f32[6,1,16]{2,0,1:T(8,128)} %copy.122) | copy-start | bytes 1156
  319.7 70.8 %copy-start.8 = (bf16[2,6,3072]{2,1,0:T(8,128)(2,1)S(1)}, bf16[2,6,3072]{2,1,0:T(8,128)(2,1)}, u32[]{:S(2)}) copy-start(bf16[2,6,3072]{2,1,0:T(8,128)(2,1)} %copy-done.7) | copy-start | bytes 221188
  319.7 70.8 %copy-start.10 = (bf16[6,3072]{1,0:T(8,128)(2,1)S(1)}, bf16[6,3072]{1,0:T(8,128)(2,1)}, u32[]{:S(2)}) copy-start(bf16[6,3072]{1,0:T(8,128)(2,1)} %copy-done.9) | copy-start | bytes 110596
  323.7 66.8 %copy-start.16 = (bf16[1,2,6,3072]{3,2,1,0:T(8,128)(2,1)S(1)}, bf16[1,2,6,3072]{3,2,1,0:T(8,128)(2,1)}, u32[]{:S(2)}) copy-start(bf16[1,2,6,3072]{3,2,1,0:T(8,128)(2,1)} %copy.130) | copy-start | bytes 221188
  375.0 12.5 %collective-permute-start.10 = (f32[8,3072]{1,0:T(8,128)S(1)}, f32[8,3072]{1,0:T(8,128)S(1)}, u32[]{:S(2)}, u32[]{:S(2)}) collective-permute-start(f32[8,3072]{1,0:T(8,128)S(1)} %fusion.2), channel_id=1, source_target_pairs={{0,1},{1,2},{2,3},{3,4},{4,5},{5,6},{6,7},{7,8},{8,9},{9,10},{10,1... | collective-permute-start | bytes 294920
  378.5 9.0 %collective-permute-start.11 = (f32[8,3072]{1,0:T(8,128)S(1)}, f32[8,3072]{1,0:T(8,128)S(1)}, u32[]{:S(2)}, u32[]{:S(2)}) collective-permute-start(f32[8,3072]{1,0:T(8,128)S(1)} %fusion.2), channel_id=1, source_target_pairs={{0,2},{1,3},{2,4},{3,5},{4,6},{5,7},{6,8},{7,9},{8,10},{9,11},{10,... | collective-permute-start | bytes 294920
  379.8 8.3 %collective-permute-start.12 = (f32[8,3072]{1,0:T(8,128)S(1)}, f32[8,3072]{1,0:T(8,128)}, u32[]{:S(2)}, u32[]{:S(2)}) collective-permute-start(f32[8,3072]{1,0:T(8,128)S(1)} %fusion.2), channel_id=1, source_target_pairs={{0,3},{1,4},{2,5},{3,6},{4,7},{5,8},{6,9},{7,10},{8,11},{9,12},{10... | collective-permute-start | bytes 294920
  381.7 5.7 %collective-permute-start.13 = (f32[6,3072]{1,0:T(8,128)S(1)}, f32[6,3072]{1,0:T(8,128)S(1)}, u32[]{:S(2)}, u32[]{:S(2)}) collective-permute-start(f32[6,3072]{1,0:T(8,128)S(1)} %slice.38), channel_id=1, source_target_pairs={{0,4},{1,5},{2,6},{3,7},{4,8},{5,9},{6,10},{7,11},{8,12},{9,13},{1... | collective-permute-start | bytes 221192
  387.4 0.6 copy-start.24
  (2 other events, 1.2 us)
